TPU v7x, 128 devices: a whole 4x4x4 slice. The times are simulated.
128 devices in a mesh: seq: 16 (over x, z), head: 8 (over y, core).
Axes of the slice: x: 4, y: 4, z: 4, core: 2. Of those that a mesh axis runs over, the one named last changes fastest.
Arguments:
- context: bfloat16 [8, 8192, 1024], P('head', 'seq'), may hold values from -6 to 6
- latents: bfloat16 [8, 1024, 1024], P('head'), may hold values from -6 to 6
- offsets: int32 [8], P('head'), may hold values from 0 to 7168
- query_gain: float32 [1024], replicated, may hold values from 0.1 to 1.9
- key_gain: float32 [1024], replicated, may hold values from 0.1 to 1.9
- layer_gain: float32 [2, 1024], replicated, may hold values from 0.1 to 1.9
- cross_query: bfloat16 [1024, 1024], P(('seq', 'head')), may hold values from -0.25 to 0.25
- cross_key: bfloat16 [1024, 1024], P(('seq', 'head')), may hold values from -0.25 to 0.25
- cross_value: bfloat16 [1024, 1024], P(('seq', 'head')), may hold values from -0.1875 to 0.1875
- cross_out: bfloat16 [1024, 1024], P(('seq', 'head')), may hold values from -0.1875 to 0.1875
- layer_qkv: bfloat16 [2, 1024, 3072], P(None, ('seq', 'head')), may hold values from -0.25 to 0.25
- layer_out: bfloat16 [2, 1024, 1024], P(None, ('seq', 'head')), may hold values from -0.1875 to 0.1875
Outputs:
- latent_out: bfloat16 [8, 1024, 1024], P('head', 'seq')
Inputs may be any that keep to these rules, and one draw needn't show every extreme that they name: Latent i of row b stands at context position offsets[b] + i.
All inputs are finite; a program needn't handle non-finite values.
Results may differ from a plain program's by a relative error of at most 0.013.
Values may be sent and summed in bfloat16 or wider, within the bound.
A program may use at most 128 MiB of HBM per device.

v0:
```python
import jax
import jax.numpy as jnp
from jax import lax
from jax.sharding import PartitionSpec as P

H = 16
EPSILON = 1e-06
NEGATIVE = -1e30


def rows_first(arrays, axis, dims):
    turned = [jnp.moveaxis(a, dim, 0) for a, dim in zip(arrays, dims)]
    widths = [t[0].size for t in turned]
    both = jnp.concatenate([t.reshape(-1, w) for t, w in zip(turned, widths)], axis=1)
    out = lax.all_gather(both, axis, axis=0, tiled=True)
    parts = jnp.split(out, [sum(widths[:k]) for k in range(1, len(widths))], axis=1)
    return tuple(
        (
            jnp.moveaxis(b.reshape(-1, *t.shape[1:]), 0, dim)
            for b, t, dim in zip(parts, turned, dims)
        )
    )


def rms_norm(value_matrix, gain):
    value_matrix = value_matrix.astype(jnp.float32)
    scale = lax.rsqrt(jnp.mean(value_matrix * value_matrix, axis=-1, keepdims=True) + EPSILON)
    return (value_matrix * scale * gain).astype(jnp.bfloat16)


def project(left, weight):
    return jnp.einsum("...k,kn->...n", left, weight, preferred_element_type=jnp.float32)


def block_scores(query_row_block, key_rows, query_pos, key_base, start, key_span, scale):
    key_tile = lax.dynamic_slice_in_dim(key_rows, start, key_span, 0)
    score_matrix = (
        jnp.einsum("oqi,cqi->qoc", query_row_block, key_tile, preferred_element_type=jnp.float32)
        * scale
    )
    key_pos = key_base + start + jnp.arange(key_span, dtype=jnp.int32)
    valid = key_pos[None, None, :] <= query_pos[None, :, None]
    return (jnp.where(valid, score_matrix, NEGATIVE), valid)


def causal_top(query_row_block, key_rows, query_pos, last_pos, key_base, key_span, scale):

    def advance(index, best):
        start = index * key_span

        def compute(kept):
            score_matrix, valid = block_scores(
                query_row_block, key_rows, query_pos, key_base, start, key_span, scale
            )
            return jnp.maximum(kept, jnp.max(score_matrix, axis=2))

        result = lax.cond(key_base + start <= last_pos, compute, lambda kept: kept, best)
        return result

    initial = jnp.full((query_row_block.shape[1], query_row_block.shape[0]), NEGATIVE, jnp.float32)
    return lax.fori_loop(0, key_rows.shape[0] // key_span, advance, initial)


def causal_sums(
    query_row_block, key_rows, value_rows, row_top, query_pos, last_pos, key_base, key_span, scale
):

    def advance(index, carry):
        start = index * key_span

        def compute(kept):
            numerator_sum, denom = kept
            score_matrix, valid = block_scores(
                query_row_block, key_rows, query_pos, key_base, start, key_span, scale
            )
            probability_rows = jnp.where(
                valid, jnp.exp(score_matrix - row_top[:, :, None]), 0.0
            ).astype(jnp.bfloat16)
            value_tile = lax.dynamic_slice_in_dim(value_rows, start, key_span, 0)
            numerator_sum = numerator_sum + jnp.einsum(
                "ycv,vys->cys", probability_rows, value_tile, preferred_element_type=jnp.float32
            )
            denom = denom + jnp.transpose(jnp.sum(probability_rows.astype(jnp.float32), axis=2))
            return (numerator_sum, denom)

        result = lax.cond(key_base + start <= last_pos, compute, lambda kept: kept, carry)
        return result

    count, heads, head_width = query_row_block.shape
    initial = (
        jnp.zeros((count, heads, head_width), jnp.float32),
        jnp.zeros((count, heads), jnp.float32),
    )
    return lax.fori_loop(0, key_rows.shape[0] // key_span, advance, initial)


def latent_attention(piece):
    count = piece.shape[1]
    head_width = piece.shape[-1]
    query_matrix = piece[:, :, 0]
    key_matrix = piece[:, :, 1]
    value_matrix = piece[:, :, 2]
    score_matrix = jnp.einsum(
        "bmhd,bkhd->bhmk", query_matrix, key_matrix, preferred_element_type=jnp.float32
    ) * head_width ** (-0.5)
    positions = jnp.arange(count, dtype=jnp.int32)
    valid = positions[None, :] <= positions[:, None]
    score_matrix = jnp.where(valid, score_matrix, NEGATIVE)
    row_top = jnp.max(score_matrix, axis=3, keepdims=True)
    probability_rows = jnp.where(valid, jnp.exp(score_matrix - row_top), 0.0).astype(jnp.bfloat16)
    denom = jnp.sum(probability_rows.astype(jnp.float32), axis=3)
    numerator_sum = jnp.einsum(
        "bhmk,bkhd->bmhd", probability_rows, value_matrix, preferred_element_type=jnp.float32
    )
    return (numerator_sum / jnp.transpose(denom, (0, 2, 1))[:, :, :, None]).astype(jnp.bfloat16)


def per_device(
    context,
    latents,
    offsets,
    query_gain,
    key_gain,
    layer_gain,
    cross_query,
    cross_key,
    cross_value,
    cross_out,
    layer_qkv,
    layer_out,
):
    batch, ctx_len, width = context.shape
    latent_count = latents.shape[1]
    heads = H
    head_width = width // heads
    groups = lax.axis_size("seq")
    local_rows = latent_count // groups
    group_heads = heads // groups
    seq_index = lax.axis_index("seq")
    scale = head_width ** (-0.5)
    gathered = rows_first(
        (cross_query, cross_key, cross_value, cross_out, layer_qkv, layer_out),
        ("seq", "head"),
        (0, 0, 0, 0, 1, 1),
    )
    normed_latents = rms_norm(latents, query_gain)
    query_matrix = project(normed_latents, gathered[0])
    query_matrix = query_matrix.astype(jnp.bfloat16)
    normed_context = rms_norm(context, key_gain)
    key_matrix = project(normed_context, gathered[1])
    value_matrix = project(normed_context, gathered[2])
    key_matrix = key_matrix.astype(jnp.bfloat16).reshape(batch, ctx_len, heads, head_width)
    value_matrix = value_matrix.astype(jnp.bfloat16).reshape(batch, ctx_len, heads, head_width)
    query_head_rows = query_matrix.reshape(batch, latent_count, heads, head_width)
    query_pos = offsets[:, None] + jnp.arange(latent_count, dtype=jnp.int32)[None, :]
    last_pos = offsets + (latent_count - 1)
    key_groups, value_groups = (
        lax.all_to_all(key_matrix, "seq", split_axis=2, concat_axis=1, tiled=True),
        lax.all_to_all(value_matrix, "seq", split_axis=2, concat_axis=1, tiled=True),
    )
    query_groups = lax.dynamic_slice_in_dim(
        query_head_rows, seq_index * group_heads, group_heads, 2
    )
    total_len = key_groups.shape[1]
    key_span = max(min(total_len, 512), total_len // 16)
    row_top = causal_top(
        query_groups[0], key_groups[0], query_pos[0], last_pos[0], 0, key_span, scale
    )
    numerator_sum, denom = causal_sums(
        query_groups[0],
        key_groups[0],
        value_groups[0],
        row_top,
        query_pos[0],
        last_pos[0],
        0,
        key_span,
        scale,
    )
    results = [(numerator_sum / denom[:, :, None]).astype(jnp.bfloat16)]
    attended = lax.all_to_all(
        jnp.stack(results), "seq", split_axis=1, concat_axis=2, tiled=True
    ).reshape(batch, local_rows, width)
    latents_own = lax.dynamic_slice_in_dim(latents, seq_index * local_rows, local_rows, 1)
    update = project(attended, gathered[3])
    hidden = (latents_own.astype(jnp.float32) + update).astype(jnp.bfloat16)
    for layer in range(layer_qkv.shape[0]):
        normed = rms_norm(hidden, layer_gain[layer])
        qkv = project(normed, gathered[4][layer])
        grouped = qkv.astype(jnp.bfloat16).reshape(batch, local_rows, 3, heads, head_width)
        mixed = latent_attention(
            lax.all_to_all(grouped, "seq", split_axis=3, concat_axis=1, tiled=True)
        )
        merged = lax.all_to_all(mixed, "seq", split_axis=1, concat_axis=2, tiled=True).reshape(
            batch, local_rows, width
        )
        update = project(merged, gathered[5][layer])
        hidden = (hidden.astype(jnp.float32) + update).astype(jnp.bfloat16)
    return hidden


def solution(mesh):
    return jax.shard_map(
        per_device,
        mesh=mesh,
        in_specs=(
            P("head", "seq", None),
            P("head", None, None),
            P("head"),
            P(),
            P(),
            P(),
            P(("seq", "head"), None),
            P(("seq", "head"), None),
            P(("seq", "head"), None),
            P(("seq", "head"), None),
            P(None, ("seq", "head"), None),
            P(None, ("seq", "head"), None),
        ),
        out_specs=P("head", "seq", None),
        check_vma=False,
    )
```

profile of v0, /device:TPU:8, one launch (start us, length us, event | category | flops | bytes accessed | tf_op | source)
XLA Modules:
  0.0 371.7 jit_solution(11216655208212201364)
XLA Ops:
  13.3 93.9 %all-gather.2.cloned.1.call-done = bf16[1024,12288]{1,0:T(8,128)(2,1)} async-done(((bf16[8,12288]{1,0:T(8,128)(2,1)}), bf16[1024,12288]{1,0:T(8,128)(2,1)}) %all-gather.2.cloned.1.call-update) | async-done | bytes 25165840 | tf_op jit(solution)/shard_map/all_gather | solution.py:15
  107.2 3.2 fusion.54
  111.8 5.1 %all-to-all-start.1 = ((bf16[1,512,16,64]{1,3,0,2:T(8,128)(2,1)}), bf16[1,512,16,64]{1,3,0,2:T(8,128)(2,1)S(1)}, u32[]{:S(2)}, u32[]{:S(2)}) async-start(bf16[1,512,16,64]{1,3,0,2:T(8,128)(2,1)} %bitcast.25), calls=%async_computation.1 | async-start | bytes 2097152 | tf_op jit(solution)/shard_map/all_to_all | solution.py:158
  116.9 2.9 fusion.51
  121.2 14.0 %all-to-all-done.1 = bf16[1,512,16,64]{1,3,0,2:T(8,128)(2,1)S(1)} async-done(((bf16[1,512,16,64]{1,3,0,2:T(8,128)(2,1)}), bf16[1,512,16,64]{1,3,0,2:T(8,128)(2,1)S(1)}, u32[]{:S(2)}, u32[]{:S(2)}) %all-to-all-start.1) | async-done | bytes 1048608 | tf_op jit(solution)/shard_map/all_to_all | solution.py:158
  135.1 3.8 %all-to-all-start = ((bf16[1,512,16,64]{1,3,0,2:T(8,128)(2,1)}), bf16[1,512,16,64]{1,3,0,2:T(8,128)(2,1)S(1)}, u32[]{:S(2)}, u32[]{:S(2)}) async-start(bf16[1,512,16,64]{1,3,0,2:T(8,128)(2,1)} %bitcast.21), calls=%async_computation | async-start | bytes 2097152 | tf_op jit(solution)/shard_map/all_to_all | solution.py:159
  141.7 4.8 %fusion.46 = bf16[1024,1024]{0,1:T(8,128)(2,1)S(1)} fusion(bf16[1024,12288]{1,0:T(8,128)(2,1)} %all-gather.2.cloned.1.call-done, bf16[1,1024,1024]{2,1,0:T(8,128)(2,1)} %param.21, f32[1024]{0:T(1024)S(1)} %copy-done.4, f32[1024]{0:T(1024)S(1)} %add_rsqrt_fusion), kind=kOutput, calls=%fused_computation.67 | convolution fusion | flops 2152726528 | bytes 6299648 | tf_op jit(solution)/shard_map/...k,kn->...n/dot_general | solution.py:32
  148.5 6.2 %all-to-all-done = bf16[1,512,16,64]{1,3,0,2:T(8,128)(2,1)S(1)} async-done(((bf16[1,512,16,64]{1,3,0,2:T(8,128)(2,1)}), bf16[1,512,16,64]{1,3,0,2:T(8,128)(2,1)S(1)}, u32[]{:S(2)}, u32[]{:S(2)}) %all-to-all-start) | async-done | bytes 1048608 | tf_op jit(solution)/shard_map/all_to_all | solution.py:159
  155.9 33.2 %while.33 = (s32[]{:T(128)}, f32[1,1024]{1,0:T(1,128)S(1)}, s32[]{:T(128)}, bf16[8192,1,64]{0,2,1:T(8,128)(2,1)}, bf16[1024,1,64]{0,2,1:T(8,128)(2,1)S(1)}, /*index=5*/s32[]{:T(128)}, s32[]{:T(128)}, s32[]{:T(128)}) while((s32[]{:T(128)}, f32[1,1024]{1,0:T(1,128)S(1)}, s32[]{:T(128)}, bf16[8192,1,64]{0,2,1:T(8,128)(2,1)}, ...), condition=%wide.region_6.7_spmd.clone, body=%wide.region_2.6_spmd.clone.sunk | while | flops 69207552 | bytes 233685 | solution.py:61
  189.2 43.4 %while.34 = (s32[]{:T(128)}, f32[1024,1,64]{0,2,1:T(8,128)S(1)}, f32[1024,1]{0,1:T(1,128)S(1)}, s32[]{:T(128)}, bf16[8192,1,64]{0,2,1:T(8,128)(2,1)S(1)}, /*inde...) while((s32[]{:T(128)}, f32[1024,1,64]{0,2,1:T(8,128)S(1)}, ...), condition=%wide.region_11.12_spmd.clone, body=%wide.region_7.11_spmd.clone.sunk | while | flops 138479104 | bytes 2924841 | solution.py:94
  189.2 2.7 conditional.7
  191.9 2.7 conditional.7
  194.7 2.7 conditional.7
  197.4 2.7 conditional.7
  202.8 2.7 conditional.7
  205.5 2.7 conditional.7
  213.6 2.7 conditional.7
  216.4 2.7 conditional.7
  224.5 2.7 conditional.7
  227.2 2.7 conditional.7
  236.7 3.8 %all-to-all-start.2 = ((bf16[16,2,2048]{2,1,0:T(2,128)(2,1)}), bf16[16,2,2048]{2,1,0:T(2,128)(2,1)S(1)}, u32[]{:S(2)}, u32[]{:S(2)}) async-start(bf16[16,2,2048]{2,1,0:T(2,128)(2,1)} %reshape.299), calls=%async_computation.2 | async-start | bytes 262144 | tf_op jit(solution)/shard_map/all_to_all | solution.py:181
  240.5 10.7 %split.28 = bf16[1024,6144]{1,0:T(8,128)(2,1)} slice(bf16[1024,12288]{1,0:T(8,128)(2,1)} %all-gather.2.cloned.1.call-done), slice={[0:1024], [4096:10240]} | slice | bytes 25165824 | tf_op jit(solution)/shard_map/split | solution.py:16
  251.2 16.6 %copy.91 = bf16[1024,6144]{0,1:T(8,128)(2,1)} copy(bf16[1024,6144]{1,0:T(8,128)(2,1)} %split.28) | data formatting | bytes 25165824
  271.4 4.8 %fusion.25 = bf16[64,3072]{1,0:T(8,128)(2,1)S(1)} fusion(bf16[2,1024,3072]{1,2,0:T(8,128)(2,1)} %bitcast.260, f32[1,64,1024]{2,1,0:T(8,128)S(1)} %get-tuple-element.412, f32[1024]{0:T(1024)S(1)} %bitcast.285, f32[64]{0:T(128)S(1)} %add_rsqrt_fusion.3), kind=kOutput, calls=%fused_computation.43 | convolution fusion | flops 403046400 | bytes 6951168 | tf_op jit(solution)/shard_map/...k,kn->...n/dot_general | solution.py:32
  278.1 16.0 %all_to_all.111 = bf16[16,2,6144]{2,1,0:T(2,128)(2,1)S(1)} all-to-all(bf16[16,2,6144]{2,1,0:T(2,128)(2,1)S(1)} %reshape.301), channel_id=1, replica_groups=mesh['seq'=16,'head'=8] {'seq'}, dimensions={0} | all-to-all | bytes 786432 | tf_op jit(solution)/shard_map/all_to_all | solution.py:192
  301.1 3.8 %all-to-all-start.4 = ((bf16[16,2,2048]{2,1,0:T(2,128)(2,1)}), bf16[16,2,2048]{2,1,0:T(2,128)(2,1)S(1)}, u32[]{:S(2)}, u32[]{:S(2)}) async-start(bf16[16,2,2048]{2,1,0:T(2,128)(2,1)} %reshape.303), calls=%async_computation.4 | async-start | bytes 262144 | tf_op jit(solution)/shard_map/all_to_all | solution.py:194
  305.0 4.7 %split.29 = bf16[1024,2048]{1,0:T(8,128)(2,1)} slice(bf16[1024,12288]{1,0:T(8,128)(2,1)} %all-gather.2.cloned.1.call-done), slice={[0:1024], [10240:12288]} | slice | bytes 8388608 | tf_op jit(solution)/shard_map/split | solution.py:16
  309.7 6.4 %copy.92 = bf16[1024,2048]{0,1:T(8,128)(2,1)} copy(bf16[1024,2048]{1,0:T(8,128)(2,1)} %split.29) | data formatting | bytes 8388608
  320.0 4.8 %fusion.26 = bf16[64,3072]{1,0:T(8,128)(2,1)S(1)} fusion(bf16[2,1024,3072]{1,2,0:T(8,128)(2,1)} %bitcast.261, f32[1,64,1024]{2,1,0:T(8,128)S(1)} %get-tuple-element.416, f32[1024]{0:T(1024)S(1)} %bitcast.284, f32[64]{0:T(128)S(1)} %add_rsqrt_fusion.2), kind=kOutput, calls=%fused_computation.44 | convolution fusion | flops 403046400 | bytes 6951168 | tf_op jit(solution)/shard_map/...k,kn->...n/dot_general | solution.py:32
  326.7 16.0 %all_to_all.112 = bf16[16,2,6144]{2,1,0:T(2,128)(2,1)S(1)} all-to-all(bf16[16,2,6144]{2,1,0:T(2,128)(2,1)S(1)} %reshape.305), channel_id=1, replica_groups=mesh['seq'=16,'head'=8] {'seq'}, dimensions={0} | all-to-all | bytes 786432 | tf_op jit(solution)/shard_map/all_to_all | solution.py:192
  349.1 11.4 %all_to_all.113 = bf16[16,2,2048]{2,1,0:T(2,128)(2,1)S(1)} all-to-all(bf16[16,2,2048]{2,1,0:T(2,128)(2,1)S(1)} %reshape.307), channel_id=1, replica_groups=mesh['seq'=16,'head'=8] {'seq'}, dimensions={0} | all-to-all | bytes 262144 | tf_op jit(solution)/shard_map/all_to_all | solution.py:194
  361.9 3.0 fusion.75
  (283 shorter events, 166.9 us)
Async XLA Ops:
  6.5 100.6 %all-gather.2.cloned.1.call-start = ((), (), s32[]{:S(2)}) async-start(), calls=%async_computation.7 | async-start | bytes 25362432 | tf_op jit(solution)/shard_map/all_gather | solution.py:15
  11.1 0.7 copy-start.1
  110.4 6.5 %copy-start = (bf16[1,512,1024]{2,1,0:T(8,128)(2,1)S(1)}, bf16[1,512,1024]{2,1,0:T(8,128)(2,1)}, u32[]{:S(2)}) copy-start(bf16[1,512,1024]{2,1,0:T(8,128)(2,1)} %param.20) | copy-start | bytes 3145732
  110.4 6.5 %copy-start.3 = (f32[1024]{0:T(1024)S(1)}, f32[1024]{0:T(1024)}, u32[]{:S(2)}) copy-start(f32[1024]{0:T(1024)} %param.24) | copy-start | bytes 12292
  111.8 23.3 %all-to-all-start.1 = ((bf16[1,512,16,64]{1,3,0,2:T(8,128)(2,1)}), bf16[1,512,16,64]{1,3,0,2:T(8,128)(2,1)S(1)}, u32[]{:S(2)}, u32[]{:S(2)}) async-start(bf16[1,512,16,64]{1,3,0,2:T(8,128)(2,1)} %bitcast.25), calls=%async_computation.1 | async-start | bytes 2097152 | tf_op jit(solution)/shard_map/all_to_all | solution.py:158
  119.8 21.9 %copy-start.4 = (f32[1024]{0:T(1024)S(1)}, f32[1024]{0:T(1024)}, u32[]{:S(2)}) copy-start(f32[1024]{0:T(1024)} %param.23) | copy-start | bytes 12292
  135.1 19.6 %all-to-all-start = ((bf16[1,512,16,64]{1,3,0,2:T(8,128)(2,1)}), bf16[1,512,16,64]{1,3,0,2:T(8,128)(2,1)S(1)}, u32[]{:S(2)}, u32[]{:S(2)}) async-start(bf16[1,512,16,64]{1,3,0,2:T(8,128)(2,1)} %bitcast.21), calls=%async_computation | async-start | bytes 2097152 | tf_op jit(solution)/shard_map/all_to_all | solution.py:159
  189.2 51.3 %copy-start.2 = (f32[2,1024]{1,0:T(2,128)S(1)}, f32[2,1024]{1,0:T(2,128)}, u32[]{:S(2)}) copy-start(f32[2,1024]{1,0:T(2,128)} %param.25) | copy-start | bytes 24580
  236.7 31.1 %all-to-all-start.2 = ((bf16[16,2,2048]{2,1,0:T(2,128)(2,1)}), bf16[16,2,2048]{2,1,0:T(2,128)(2,1)S(1)}, u32[]{:S(2)}, u32[]{:S(2)}) async-start(bf16[16,2,2048]{2,1,0:T(2,128)(2,1)} %reshape.299), calls=%async_computation.2 | async-start | bytes 262144 | tf_op jit(solution)/shard_map/all_to_all | solution.py:181
  301.1 14.9 %all-to-all-start.4 = ((bf16[16,2,2048]{2,1,0:T(2,128)(2,1)}), bf16[16,2,2048]{2,1,0:T(2,128)(2,1)S(1)}, u32[]{:S(2)}, u32[]{:S(2)}) async-start(bf16[16,2,2048]{2,1,0:T(2,128)(2,1)} %reshape.303), calls=%async_computation.4 | async-start | bytes 262144 | tf_op jit(solution)/shard_map/all_to_all | solution.py:194
Sparse Core Ops, SparseCore 0:
  11.9 95.2 all-gather.1
where the time goes:
time: 375 us; the launch traced here: 372 us
  waiting for transfers between devices  114 us (30%)
  matrix products  82.9 us (22%)
  local copies, waits for them, and re-layouts  64.5 us (17%)
  blocking collectives  43.4 us (12%)
  other arithmetic  33 us (9%)
  starting transfers between devices  16.5 us (4%)
  between operations  14.6 us (4%)
    all_gather x1, waiting for transfers between devices, rows_first(): out = lax.all_gather(both, axis, axis=0, tiled=True)  93.9 us
    dot_general x32, matrix products, block_scores(): jnp.einsum('oqi,cqi->qoc', query_row_block, key_tile, preferred_element_t...  47.2 us
    unnamed x28, local copies, waits for them, and re-layouts  33.1 us
    all_to_all x2, blocking collectives, per_device(): lax.all_to_all(grouped, 'seq', split_axis=3, concat_axis=1, tiled=True)  32 us
    dot_general x8, matrix products, project(): jnp.einsum('...k,kn->...n', left, weight, preferred_element_type=jnp.floa...  28.2 us
    add x32, other arithmetic, per_device(): offsets[:, None] + jnp.arange(latent_count, dtype=jnp.int32)[None, :]  20.9 us
    split x2, local copies, waits for them, and re-layouts, rows_first(): jnp.split(out, [sum(widths[:k]) for k in range(1, len(widths))], axis=1)  15.4 us
    all_to_all x1, waiting for transfers between devices, per_device(): lax.all_to_all(key_matrix, 'seq', split_axis=2, concat_axis=1, tiled=True)  14 us
  transfers between devices with their start and end apart: 5, of which 3 were waited for; matrix products, arithmetic and copies ran while one was open for 14% of the time, Pallas kernels for 0%

commit v1 on v0

--- a/solution.py
+++ b/solution.py
@@ -2,6 +2,7 @@
 import jax.numpy as jnp
 from jax import lax
 from jax.sharding import PartitionSpec as P
+from jax.lax import all_to_all, axis_size
 
 H = 16
 EPSILON = 1e-06
@@ -12,7 +13,9 @@
     turned = [jnp.moveaxis(a, dim, 0) for a, dim in zip(arrays, dims)]
     widths = [t[0].size for t in turned]
     both = jnp.concatenate([t.reshape(-1, w) for t, w in zip(turned, widths)], axis=1)
-    out = lax.all_gather(both, axis, axis=0, tiled=True)
+    out = jnp.concatenate(
+        all_to_all(jnp.stack(tuple((both for _ in range(axis_size(axis))))), axis, 0, 0), axis=0
+    )
     parts = jnp.split(out, [sum(widths[:k]) for k in range(1, len(widths))], axis=1)
     return tuple(
         (

time: 375 us -> 664 us (1.77)
  the two profiles are of different devices: /device:TPU:8 before, /device:TPU:16 now
where the time goes in v1:
time: 664 us; the launch traced here: 658 us
  waiting for transfers between devices  377 us (57%)
  local copies, waits for them, and re-layouts  72.7 us (11%)
  matrix products  69.4 us (10%)
  starting transfers between devices  58.2 us (9%)
  blocking collectives  44.9 us (7%)
  other arithmetic  31.7 us (5%)
    all_to_all x1, waiting for transfers between devices, rows_first(): all_to_all(jnp.stack(tuple((both for _ in range(axis_size(axis))))), axis...  364 us
    split x4, local copies, waits for them, and re-layouts, rows_first(): jnp.split(out, [sum(widths[:k]) for k in range(1, len(widths))], axis=1)  38.4 us
    dot_general x32, matrix products, block_scores(): jnp.einsum('oqi,cqi->qoc', query_row_block, key_tile, preferred_element_t...  34 us
    all_to_all x2, blocking collectives, per_device(): lax.all_to_all(grouped, 'seq', split_axis=3, concat_axis=1, tiled=True)  33.6 us
    all_to_all x1, starting transfers between devices, per_device(): lax.all_to_all(key_matrix, 'seq', split_axis=2, concat_axis=1, tiled=True)  31.3 us
    dot_general x8, matrix products, project(): jnp.einsum('...k,kn->...n', left, weight, preferred_element_type=jnp.floa...  27.9 us
    add x32, other arithmetic, per_device(): offsets[:, None] + jnp.arange(latent_count, dtype=jnp.int32)[None, :]  20.9 us
  transfers between devices with their start and end apart: 5, of which 2 were waited for; matrix products, arithmetic and copies ran while one was open for 11% of the time, Pallas kernels for 0%

profile of v1, /device:TPU:16, one launch (start us, length us, event | category | flops | bytes accessed | tf_op | source)
XLA Modules:
  0.0 658.1 jit_solution(10617318229582156548)
XLA Ops:
  4.5 8.7 %stack.4 = bf16[128,8,12288]{2,1,0:T(8,128)(2,1)} broadcast(bf16[8,12288]{1,0:T(8,128)(2,1)S(1)} %constant_dynamic-update-slice_fusion), dimensions={1,2} | broadcast | bytes 25362432 | tf_op jit(solution)/shard_map/stack | solution.py:17
  13.2 10.7 %all-to-all-start = ((bf16[128,8,12288]{2,1,0:T(8,128)(2,1)}), bf16[128,8,12288]{2,1,0:T(8,128)(2,1)}, u32[]{:S(2)}, u32[]{:S(2)}) async-start(bf16[128,8,12288]{2,1,0:T(8,128)(2,1)} %stack.4), calls=%async_computation | async-start | bytes 50331648 | tf_op jit(solution)/shard_map/all_to_all | solution.py:17
  24.3 364.0 %all-to-all-done = bf16[128,8,12288]{2,1,0:T(8,128)(2,1)} async-done(((bf16[128,8,12288]{2,1,0:T(8,128)(2,1)}), bf16[128,8,12288]{2,1,0:T(8,128)(2,1)}, u32[]{:S(2)}, u32[]{:S(2)}) %all-to-all-start) | async-done | bytes 25165856 | tf_op jit(solution)/shard_map/all_to_all | solution.py:17
  388.2 2.9 fusion.54
  392.5 31.3 %all-to-all-start.2 = ((bf16[1,512,16,64]{1,3,0,2:T(8,128)(2,1)}), bf16[1,512,16,64]{1,3,0,2:T(8,128)(2,1)S(1)}, u32[]{:S(2)}, u32[]{:S(2)}) async-start(bf16[1,512,16,64]{1,3,0,2:T(8,128)(2,1)} %bitcast.26), calls=%async_computation.2 | async-start | bytes 2097152 | tf_op jit(solution)/shard_map/all_to_all | solution.py:161
  423.8 2.9 fusion.51
  428.0 13.1 %all-to-all-done.2 = bf16[1,512,16,64]{1,3,0,2:T(8,128)(2,1)S(1)} async-done(((bf16[1,512,16,64]{1,3,0,2:T(8,128)(2,1)}), bf16[1,512,16,64]{1,3,0,2:T(8,128)(2,1)S(1)}, u32[]{:S(2)}, u32[]{:S(2)}) %all-to-all-start.2) | async-done | bytes 1048608 | tf_op jit(solution)/shard_map/all_to_all | solution.py:161
  441.2 4.1 all-to-all-start.1
  448.0 4.8 fusion.46
  454.0 19.9 %while.33 = (s32[]{:T(128)}, f32[1,1024]{1,0:T(1,128)S(1)}, s32[]{:T(128)}, bf16[8192,1,64]{0,2,1:T(8,128)(2,1)S(1)}, bf16[1024,1,64]{0,2,1:T(8,128)(2,1)S(1)}, /*index=5*/s32[]{:T(128)}, s32[]{:T(128)}, s32[]{:T(128)}) while((s32[]{:T(128)}, f32[1,1024]{1,0:T(1,128)S(1)}, s32[]{:T(128)}, bf16[8192,1,64]{0,2,1:T(8,128)(2,1)S(1)}, ...), condition=%wide.region_6.7_spmd.clone, body=%wide.region_2.6_spmd.clone.sunk | while | flops 69207552 | bytes 233685 | solution.py:64
  476.1 43.5 %while.34 = (s32[]{:T(128)}, f32[1024,1,64]{0,2,1:T(8,128)S(1)}, f32[1024,1]{0,1:T(1,128)S(1)}, s32[]{:T(128)}, bf16[8192,1,64]{0,2,1:T(8,128)(2,1)S(1)}, /*inde...) while((s32[]{:T(128)}, f32[1024,1,64]{0,2,1:T(8,128)S(1)}, ...), condition=%wide.region_11.12_spmd.clone, body=%wide.region_7.11_spmd.clone.sunk | while | flops 138479104 | bytes 2924841 | solution.py:97
  478.9 2.7 conditional.7
  481.6 2.7 conditional.7
  484.3 2.7 conditional.7
  495.1 2.7 conditional.7
  497.9 2.7 conditional.7
  500.6 2.7 conditional.7
  511.4 2.7 conditional.7
  514.2 2.7 conditional.7
  516.9 2.7 conditional.7
  523.7 7.4 %all-to-all-start.3 = ((bf16[16,2,2048]{2,1,0:T(2,128)(2,1)}), bf16[16,2,2048]{2,1,0:T(2,128)(2,1)S(1)}, u32[]{:S(2)}, u32[]{:S(2)}) async-start(bf16[16,2,2048]{2,1,0:T(2,128)(2,1)} %reshape.305), calls=%async_computation.3 | async-start | bytes 262144 | tf_op jit(solution)/shard_map/all_to_all | solution.py:184
  531.1 10.7 %split.28 = bf16[1024,6144]{1,0:T(8,128)(2,1)} slice(bf16[1024,12288]{1,0:T(8,128)(2,1)} %bitcast.20), slice={[0:1024], [4096:10240]} | slice | bytes 25165824 | tf_op jit(solution)/shard_map/split | solution.py:19
  541.8 16.6 %copy.88 = bf16[1024,6144]{0,1:T(8,128)(2,1)} copy(bf16[1024,6144]{1,0:T(8,128)(2,1)} %split.28) | data formatting | bytes 25165824 | tf_op jit(solution)/shard_map/split | solution.py:19
  562.1 4.8 fusion.25
  568.8 17.3 %all_to_all.116 = bf16[16,2,6144]{2,1,0:T(2,128)(2,1)S(1)} all-to-all(bf16[16,2,6144]{2,1,0:T(2,128)(2,1)S(1)} %reshape.307), channel_id=1, replica_groups=mesh['seq'=16,'head'=8] {'seq'}, dimensions={0} | all-to-all | bytes 786432 | tf_op jit(solution)/shard_map/all_to_all | solution.py:195
  593.1 4.6 all-to-all-start.5
  597.7 4.7 split.29
  602.5 6.4 copy.95
  612.8 4.8 fusion.26
  619.4 16.2 %all_to_all.117 = bf16[16,2,6144]{2,1,0:T(2,128)(2,1)S(1)} all-to-all(bf16[16,2,6144]{2,1,0:T(2,128)(2,1)S(1)} %reshape.311), channel_id=1, replica_groups=mesh['seq'=16,'head'=8] {'seq'}, dimensions={0} | all-to-all | bytes 786432 | tf_op jit(solution)/shard_map/all_to_all | solution.py:195
  642.1 11.4 %all_to_all.118 = bf16[16,2,2048]{2,1,0:T(2,128)(2,1)S(1)} all-to-all(bf16[16,2,2048]{2,1,0:T(2,128)(2,1)S(1)} %reshape.313), channel_id=1, replica_groups=mesh['seq'=16,'head'=8] {'seq'}, dimensions={0} | all-to-all | bytes 262144 | tf_op jit(solution)/shard_map/all_to_all | solution.py:197
  654.9 3.0 fusion.75
  (283 shorter events, 141.3 us)
Async XLA Ops:
  13.2 10.8 %copy-start = (bf16[1,512,1024]{2,1,0:T(8,128)(2,1)S(1)}, bf16[1,512,1024]{2,1,0:T(8,128)(2,1)}, u32[]{:S(2)}) copy-start(bf16[1,512,1024]{2,1,0:T(8,128)(2,1)} %param.20) | copy-start | bytes 3145732
  13.2 375.0 %copy-start.3 = (f32[1024]{0:T(1024)S(1)}, f32[1024]{0:T(1024)}, u32[]{:S(2)}) copy-start(f32[1024]{0:T(1024)} %param.24) | copy-start | bytes 12292
  13.2 375.0 %all-to-all-start = ((bf16[128,8,12288]{2,1,0:T(8,128)(2,1)}), bf16[128,8,12288]{2,1,0:T(8,128)(2,1)}, u32[]{:S(2)}, u32[]{:S(2)}) async-start(bf16[128,8,12288]{2,1,0:T(8,128)(2,1)} %stack.4), calls=%async_computation | async-start | bytes 50331648 | tf_op jit(solution)/shard_map/all_to_all | solution.py:17
  392.5 48.6 %all-to-all-start.2 = ((bf16[1,512,16,64]{1,3,0,2:T(8,128)(2,1)}), bf16[1,512,16,64]{1,3,0,2:T(8,128)(2,1)S(1)}, u32[]{:S(2)}, u32[]{:S(2)}) async-start(bf16[1,512,16,64]{1,3,0,2:T(8,128)(2,1)} %bitcast.26), calls=%async_computation.2 | async-start | bytes 2097152 | tf_op jit(solution)/shard_map/all_to_all | solution.py:161
  426.7 21.3 %copy-start.4 = (f32[1024]{0:T(1024)S(1)}, f32[1024]{0:T(1024)}, u32[]{:S(2)}) copy-start(f32[1024]{0:T(1024)} %param.23) | copy-start | bytes 12292
  441.2 32.7 %all-to-all-start.1 = ((bf16[1,512,16,64]{1,3,0,2:T(8,128)(2,1)}), bf16[1,512,16,64]{1,3,0,2:T(8,128)(2,1)S(1)}, u32[]{:S(2)}, u32[]{:S(2)}) async-start(bf16[1,512,16,64]{1,3,0,2:T(8,128)(2,1)} %bitcast.22), calls=%async_computation.1 | async-start | bytes 2097152 | tf_op jit(solution)/shard_map/all_to_all | solution.py:162
  473.9 1.1 copy-start.1
  476.1 55.0 %copy-start.2 = (f32[2,1024]{1,0:T(2,128)S(1)}, f32[2,1024]{1,0:T(2,128)}, u32[]{:S(2)}) copy-start(f32[2,1024]{1,0:T(2,128)} %param.25) | copy-start | bytes 24580
  523.7 34.8 %all-to-all-start.3 = ((bf16[16,2,2048]{2,1,0:T(2,128)(2,1)}), bf16[16,2,2048]{2,1,0:T(2,128)(2,1)S(1)}, u32[]{:S(2)}, u32[]{:S(2)}) async-start(bf16[16,2,2048]{2,1,0:T(2,128)(2,1)} %reshape.305), calls=%async_computation.3 | async-start | bytes 262144 | tf_op jit(solution)/shard_map/all_to_all | solution.py:184
  593.1 15.7 %all-to-all-start.5 = ((bf16[16,2,2048]{2,1,0:T(2,128)(2,1)}), bf16[16,2,2048]{2,1,0:T(2,128)(2,1)S(1)}, u32[]{:S(2)}, u32[]{:S(2)}) async-start(bf16[16,2,2048]{2,1,0:T(2,128)(2,1)} %reshape.309), calls=%async_computation.5 | async-start | bytes 262144 | tf_op jit(solution)/shard_map/all_to_all | solution.py:197
